TPU v7x, 32 devices: a whole 2x2x4 slice. The times are simulated.
32 devices in a mesh: grp: 4 (over y, x), mem: 8 (over z, core).
Axes of the slice: x: 2, y: 2, z: 4, core: 2. Of those that a mesh axis runs over, the one named last changes fastest.
Arguments:
- weight: bfloat16 [2, 16384, 16384], P(None, None, ('grp', 'mem')), may hold values from -0.046875 to 0.046875
- activation: bfloat16 [2, 16384, 512], P(None, ('grp', 'mem')), may hold values from -6 to 6
- points: int32 [4], replicated, may hold values from 0 to 3, each once
Outputs:
- share: float32 [4, 16384, 512], P('grp', 'mem')
Inputs may be any that keep to these rules, and one draw needn't show every extreme that they name: A permutation of 0 to 3; group g evaluates at points[g] + 1.
All inputs are finite; a program needn't handle non-finite values.
Results may differ from a plain program's by a relative error of at most 0.0042.
Values may be sent and summed in bfloat16 or wider, within the bound.
A program may use at most 320 MiB of HBM per device.

v0:
```python
import jax
import jax.numpy as jnp
from jax import lax
from jax.sharding import PartitionSpec as P


def code_stack(raw_blocks, factors):
    total = factors[:, 0, None, None] * raw_blocks[0].astype(jnp.float32)[None]
    for block in range(1, raw_blocks.shape[0]):
        total = total + factors[:, block, None, None] * raw_blocks[block].astype(jnp.float32)[None]
    return total.astype(jnp.bfloat16)


def per_device(weight, activation, points):
    groups = lax.axis_size("grp")
    blocks = weight.shape[0]
    splits = activation.shape[0]
    anchors = (points + 1).astype(jnp.float32) / groups
    factors = anchors[:, None] ** jnp.arange(blocks, dtype=jnp.float32)[None, :]
    lifts_all = anchors[:, None] ** (jnp.arange(splits, dtype=jnp.float32) * blocks)[None, :]
    slab = lax.all_to_all(weight, "mem", split_axis=1, concat_axis=2, tiled=True)
    block_input = lax.all_gather(activation, "mem", axis=1, tiled=True)
    coded_weight = code_stack(slab, factors)
    coded_input = code_stack(block_input, lifts_all)
    return lax.psum_scatter(
        jnp.einsum("grk,gkc->grc", coded_weight, coded_input, preferred_element_type=jnp.float32),
        "grp",
        scatter_dimension=0,
        tiled=True,
    )


def solution(mesh):
    placed = (P(None, None, ("grp", "mem")), P(None, ("grp", "mem"), None), P())
    return jax.shard_map(
        per_device, mesh=mesh, in_specs=placed, out_specs=P("grp", "mem", None), check_vma=False
    )
```

profile of v0, /device:TPU:0, one launch (start us, length us, event | category | flops | bytes accessed | tf_op | source)
XLA Modules:
  0.0 1254.2 jit_solution(2382327408538441488)
XLA Ops:
  6.5 60.1 %copy.10 = bf16[2,16384,512]{2,0,1:T(2,128)(2,1)} copy(bf16[2,16384,512]{2,1,0:T(8,128)(2,1)} %param.3) | data formatting | bytes 67108864 | tf_op args[0]
  66.6 0.0 copy-start
  66.6 7.2 all-to-all-start
  73.9 0.0 all-gather.2.cloned.1.call-start
  73.9 0.7 all-gather.2.cloned.1.call-update
  74.6 0.0 reduce-scatter.4.cloned.1.call-start
  74.7 0.0 copy-done
  74.7 0.1 broadcast_power_fusion
  74.8 154.4 %all-gather.2.cloned.1.call-done = bf16[2,4096,512]{2,1,0:T(8,128)(2,1)} async-done(((bf16[2,512,512]{2,1,0:T(8,128)(2,1)}), bf16[2,4096,512]{2,1,0:T(8,128)(2,1)}) %all-gather.2.cloned.1.call-update) | async-done | bytes 8388624 | tf_op jit(solution)/shard_map/all_gather | solution.py:22
  229.1 11.7 fusion.10
  240.9 15.1 %add_convert_fusion.10 = bf16[4,4096,512]{2,1,0:T(8,128)(2,1)} fusion(f32[4096,512]{1,0:T(8,128)} %get-tuple-element.8, f32[4]{0:T(128)S(1)} %get-tuple-element.10, f32[4096,512]{1,0:T(8,128)} %get-tuple-element.7, f32[4]{0:T(128)S(1)} %get-tuple-element.9), kind=kLoop, calls=%fused_computation.6.clone.clone.2 | loop fusion | flops 33554432 | bytes 33554464 | tf_op jit(solution)/shard_map/grk,gkc->grc/dot_general | solution.py:26
  256.0 609.3 %all-to-all-done = bf16[2,16384,512]{2,0,1:T(2,128)(2,1)} async-done(((bf16[2,16384,512]{2,0,1:T(2,128)(2,1)}), bf16[2,16384,512]{2,0,1:T(2,128)(2,1)}, u32[]{:S(2)}, u32[]{:S(2)}) %all-to-all-start) | async-done | bytes 33554464 | tf_op jit(solution)/shard_map/all_to_all | solution.py:21
  865.3 22.7 %copy.11 = bf16[2,16384,512]{2,1,0:T(8,128)(2,1)} copy(bf16[2,16384,512]{2,0,1:T(2,128)(2,1)} %all-to-all-done) | data formatting | bytes 67108864 | tf_op jit(solution)/shard_map/all_to_all | solution.py:21
  888.0 34.1 %slice_convert_fusion.1 = (f32[1,2048,8,512]{3,1,2,0:T(8,128)}, f32[1,2048,8,512]{3,1,2,0:T(8,128)}) fusion(bf16[2,2048,8,512]{3,1,2,0:T(8,128)(2,1)} %bitcast.25), kind=kLoop, calls=%fused_computation.8 | loop fusion | flops 16777216 | bytes 100663296 | tf_op jit(solution)/shard_map/convert_element_type | solution.py:8
  922.1 31.8 %copy.14 = f32[1,2048,8,512]{1,3,2,0:T(8,128)} copy(f32[1,2048,8,512]{3,1,2,0:T(8,128)} %get-tuple-element.6) | data formatting | bytes 67108864 | tf_op jit(solution)/shard_map/convert_element_type | solution.py:10
  953.9 31.1 %copy.15 = f32[2048,4096]{1,0:T(8,128)} copy(f32[2048,4096]{0,1:T(8,128)} %bitcast.26) | data formatting | bytes 67108864 | tf_op jit(solution)/shard_map/convert_element_type | solution.py:10
  985.0 31.8 %copy.12 = f32[1,2048,8,512]{1,3,2,0:T(8,128)} copy(f32[1,2048,8,512]{3,1,2,0:T(8,128)} %get-tuple-element.5) | data formatting | bytes 67108864 | tf_op jit(solution)/shard_map/convert_element_type | solution.py:8
  1016.8 31.1 %copy.13 = f32[2048,4096]{1,0:T(8,128)} copy(f32[2048,4096]{0,1:T(8,128)} %bitcast.27) | data formatting | bytes 67108864 | tf_op jit(solution)/shard_map/convert_element_type | solution.py:8
  1047.9 46.0 %fusion = f32[4,2048,512]{2,1,0:T(8,128)} fusion(f32[2048,4096]{1,0:T(8,128)} %copy.15, f32[4]{0:T(128)S(1)} %get-tuple-element.15, f32[2048,4096]{1,0:T(8,128)} %copy.13, f32[4]{0:T(128)S(1)} %get-tuple-element.16, bf16[4,4096,512]{2,1,0:T(8,128)(2,1)} %add_convert_fusion.10), kind=kOutput, calls=%fused_computation.1 | convolution fusion | flops 34493956096 | bytes 100663328 | tf_op jit(solution)/shard_map/grk,gkc->grc/dot_general | solution.py:26
  1093.9 0.0 reduce-scatter.4.cloned.1.call-update
  1094.0 153.4 %reduce-scatter.4.cloned.1.call-done = f32[1,2048,512]{2,1,0:T(8,128)} async-done(((f32[4,2048,512]{2,1,0:T(8,128)}), f32[1,2048,512]{2,1,0:T(8,128)}) %reduce-scatter.4.cloned.1.call-update) | async-done | bytes 4194320
  (3 shorter events, 0.0 us)
Async XLA Ops:
  66.6 8.0 copy-start
  66.6 798.7 %all-to-all-start = ((bf16[2,16384,512]{2,0,1:T(2,128)(2,1)}), bf16[2,16384,512]{2,0,1:T(2,128)(2,1)}, u32[]{:S(2)}, u32[]{:S(2)}) async-start(bf16[2,16384,512]{2,0,1:T(2,128)(2,1)} %copy.10), calls=%async_computation | async-start | bytes 67108864 | tf_op jit(solution)/shard_map/all_to_all | solution.py:21
  73.9 155.3 %all-gather.2.cloned.1.call-start = ((), (), s32[]{:S(2)}) async-start(), calls=%async_computation.2 | async-start | bytes 9437184 | tf_op jit(solution)/shard_map/all_gather | solution.py:22
  74.6 1172.8 %reduce-scatter.4.cloned.1.call-start = ((), (), s32[]{:S(2)}) async-start(), calls=%async_computation.3 | async-start | bytes 20971520
Sparse Core Ops, SparseCore 0:
  76.3 152.8 all-gather.1
  1094.1 153.2 reduce-scatter.3
where the time goes:
time: 1260 us; the launch traced here: 1250 us
  waiting for transfers between devices  918 us (73%)
  local copies, waits for them, and re-layouts  209 us (17%)
  other arithmetic  60.9 us (5%)
  matrix products  46 us (4%)
  between operations  13.5 us (1%)
    all_to_all x1, waiting for transfers between devices, per_device(): lax.all_to_all(weight, 'mem', split_axis=1, concat_axis=2, tiled=True)  609 us
    all_gather x1, waiting for transfers between devices, per_device(): block_input = lax.all_gather(activation, 'mem', axis=1, tiled=True)  154 us
    unnamed x3, waiting for transfers between devices  154 us
    convert_element_type x2, local copies, waits for them, and re-layouts, code_stack(): raw_blocks[block].astype(jnp.float32)[None]  62.9 us
    convert_element_type x2, local copies, waits for them, and re-layouts, code_stack(): total = factors[:, 0, None, None] * raw_blocks[0].astype(jnp.float32)[None]  62.9 us
    unnamed x3, local copies, waits for them, and re-layouts  60.1 us
    dot_general x1, matrix products, per_device(): jnp.einsum('grk,gkc->grc', coded_weight, coded_input, preferred_element_t...  46 us
    convert_element_type x1, other arithmetic, code_stack(): total = factors[:, 0, None, None] * raw_blocks[0].astype(jnp.float32)[None]  34.1 us
  transfers between devices with their start and end apart: 3, of which 3 were waited for; matrix products, arithmetic and copies ran while one was open for 2% of the time, Pallas kernels for 0%

commit v1 on v0

--- a/solution.py
+++ b/solution.py
@@ -2,6 +2,25 @@
 import jax.numpy as jnp
 from jax import lax
 from jax.sharding import PartitionSpec as P
+
+
+def touch_spot_here(here_x, comm_axis):
+    axis_total = lax.psum(1, comm_axis)
+    pile = []
+    for num in range(1, axis_total):
+        pile.append((num - 1, num))
+    u_next = pile + [(axis_total - 1, 0)]
+    step_out = here_x
+    rows = [step_out]
+    for _ in range(axis_total - 1):
+        step_out = lax.ppermute(step_out, comm_axis, u_next)
+        rows += [step_out]
+    block_now = jnp.roll(
+        jnp.concatenate([*reversed(rows)], axis=1),
+        (lax.axis_index(comm_axis) + 1) * step_out.shape[1],
+        1,
+    )
+    return block_now
 
 
 def code_stack(raw_blocks, factors):
@@ -19,7 +38,7 @@
     factors = anchors[:, None] ** jnp.arange(blocks, dtype=jnp.float32)[None, :]
     lifts_all = anchors[:, None] ** (jnp.arange(splits, dtype=jnp.float32) * blocks)[None, :]
     slab = lax.all_to_all(weight, "mem", split_axis=1, concat_axis=2, tiled=True)
-    block_input = lax.all_gather(activation, "mem", axis=1, tiled=True)
+    block_input = touch_spot_here(activation, "mem")
     coded_weight = code_stack(slab, factors)
     coded_input = code_stack(block_input, lifts_all)
     return lax.psum_scatter(

time: 1260 us -> 1340 us (1.063)
  starting transfers between devices: 7.3 us -> 195 us
  waiting for transfers between devices: 918 us -> 785 us
  local copies, waits for them, and re-layouts: 209 us -> 237 us
    ppermute x0 -> x7, waiting for transfers between devices: none -> 610 us  [touch_spot_here(): step_out = lax.ppermute(step_out, comm_axis, u_next)]
    all_to_all x1, waiting for transfers between devices: 609 us -> 0.01 us  [per_device(): lax.all_to_all(weight, 'mem', split_axis=1, concat_axis=2, tiled=True)]
    ppermute x0 -> x7, starting transfers between devices: none -> 188 us  [touch_spot_here(): step_out = lax.ppermute(step_out, comm_axis, u_next)]
    all_gather x1 -> x0, waiting for transfers between devices: 154 us -> none  [per_device(): block_input = lax.all_gather(activation, 'mem', axis=1, tiled=True)]
    unnamed x3 -> x32, local copies, waits for them, and re-layouts: 60.1 us -> 87.2 us
    unnamed x3 -> x2, waiting for transfers between devices: 154 us -> 175 us
  transfers between devices with their start and end apart: 3 -> 9, of which waited for: 3 -> 8; matrix products, arithmetic and copies ran while one was open for 2% -> 4% of each run, Pallas kernels for 0% -> 0%
where the time goes in v1:
time: 1340 us
  waiting for transfers between devices  785 us (59%)
  local copies, waits for them, and re-layouts  237 us (18%)
  starting transfers between devices  195 us (15%)
  other arithmetic  60.9 us (5%)
  matrix products  46.1 us (3%)
  between operations  13.5 us (1%)
    ppermute x7, waiting for transfers between devices, touch_spot_here(): step_out = lax.ppermute(step_out, comm_axis, u_next)  610 us
    ppermute x7, starting transfers between devices, touch_spot_here(): step_out = lax.ppermute(step_out, comm_axis, u_next)  188 us
    unnamed x2, waiting for transfers between devices  175 us
    unnamed x32, local copies, waits for them, and re-layouts  87.2 us
    convert_element_type x2, local copies, waits for them, and re-layouts, code_stack(): raw_blocks[block].astype(jnp.float32)[None]  63 us
    convert_element_type x2, local copies, waits for them, and re-layouts, code_stack(): total = factors[:, 0, None, None] * raw_blocks[0].astype(jnp.float32)[None]  62.9 us
    dot_general x1, matrix products, per_device(): jnp.einsum('grk,gkc->grc', coded_weight, coded_input, preferred_element_t...  46.1 us
    convert_element_type x1, other arithmetic, code_stack(): total = factors[:, 0, None, None] * raw_blocks[0].astype(jnp.float32)[None]  34.1 us
  transfers between devices with their start and end apart: 9, of which 8 were waited for; matrix products, arithmetic and copies ran while one was open for 4% of the time, Pallas kernels for 0%

profile of v1, /device:TPU:0, one launch (start us, length us, event | category | flops | bytes accessed | tf_op | source)
XLA Modules:
  0.0 1338.0 jit_solution(12676553135009281391)
XLA Ops:
  6.5 60.1 %copy.10 = bf16[2,16384,512]{2,0,1:T(2,128)(2,1)} copy(bf16[2,16384,512]{2,1,0:T(8,128)(2,1)} %param.3) | data formatting | bytes 67108864 | tf_op args[0]
  66.6 0.0 copy-start
  66.6 0.0 copy-start.7
  66.6 7.2 all-to-all-start
  73.9 0.0 reduce-scatter.4.cloned.1.call-start
  73.9 0.0 copy-done
  73.9 0.5 collective-permute-start
  74.5 555.9 %collective-permute-done = bf16[2,512,512]{2,1,0:T(8,128)(2,1)S(1)} collective-permute-done((bf16[2,512,512]{2,1,0:T(8,128)(2,1)S(1)}, bf16[2,512,512]{2,1,0:T(8,128)(2,1)S(1)}, u32[]{:S(2)}, u32[]{:S(2)}) %collective-permute-start) | collective-permute-done | bytes 1048608 | tf_op jit(solution)/shard_map/ppermute | solution.py:16
  630.4 0.0 collective-permute-start.1
  630.4 16.1 %collective-permute-done.1 = bf16[2,512,512]{2,1,0:T(8,128)(2,1)S(1)} collective-permute-done((bf16[2,512,512]{2,1,0:T(8,128)(2,1)S(1)}, bf16[2,512,512]{2,1,0:T(8,128)(2,1)S(1)}, u32[]{:S(2)}, u32[]{:S(2)}) %collective-permute-start.1) | collective-permute-done | bytes 1048608 | tf_op jit(solution)/shard_map/ppermute | solution.py:16
  646.5 0.0 collective-permute-start.2
  646.5 16.1 %collective-permute-done.2 = bf16[2,512,512]{2,1,0:T(8,128)(2,1)S(1)} collective-permute-done((bf16[2,512,512]{2,1,0:T(8,128)(2,1)S(1)}, bf16[2,512,512]{2,1,0:T(8,128)(2,1)S(1)}, u32[]{:S(2)}, u32[]{:S(2)}) %collective-permute-start.2) | collective-permute-done | bytes 1048608 | tf_op jit(solution)/shard_map/ppermute | solution.py:16
  662.6 0.0 copy-start.1
  662.6 1.0 copy-done.1
  663.6 158.3 %collective-permute-start.3 = (bf16[2,512,512]{2,1,0:T(8,128)(2,1)S(1)}, bf16[2,512,512]{2,1,0:T(8,128)(2,1)S(1)}, u32[]{:S(2)}, u32[]{:S(2)}) collective-permute-start(bf16[2,512,512]{2,1,0:T(8,128)(2,1)S(1)} %collective-permute-done.2), channel_id=1, source_target_pairs={{0,1},{1,2},{2,3},{3,4},{4,5},{5,6},{6,7},{7,0},{8,9},{9,10},{10,1... | collective-permute-start | bytes 3145736 | tf_op jit(solution)/shard_map/ppermute | solution.py:16
  821.9 2.3 collective-permute-done.3
  824.2 0.0 copy-start.3
  824.2 1.0 copy-done.3
  825.2 11.9 collective-permute-start.4
  837.1 4.5 collective-permute-done.4
  841.6 0.0 copy-start.5
  841.6 1.0 copy-done.5
  842.6 9.7 collective-permute-start.5
  852.3 6.5 collective-permute-done.5
  858.8 7.7 collective-permute-start.6
  866.5 0.0 copy-start.6
  866.5 0.0 copy-start.4
  866.5 0.0 copy-start.2
  866.5 0.0 copy-done.7
  866.6 0.1 broadcast_power_fusion
  866.7 8.6 collective-permute-done.6
  875.2 2.3 constant_dynamic-update-slice_fusion.15
  877.5 2.3 constant_dynamic-update-slice_fusion.14
  879.8 2.3 constant_dynamic-update-slice_fusion.13
  882.1 2.3 constant_dynamic-update-slice_fusion.12
  884.3 2.3 constant_dynamic-update-slice_fusion.11
  886.6 1.0 constant_dynamic-update-slice_fusion.10
  887.6 1.0 constant_dynamic-update-slice_fusion.9
  888.7 1.0 constant_dynamic-update-slice_fusion.8
  889.7 2.3 constant_dynamic-update-slice_fusion.7
  892.0 2.3 constant_dynamic-update-slice_fusion.6
  894.3 0.0 copy-done.6
  894.3 1.0 constant_dynamic-update-slice_fusion.5
  895.3 0.0 copy-done.4
  895.3 1.0 constant_dynamic-update-slice_fusion.4
  896.4 0.0 copy-done.2
  896.4 1.0 constant_dynamic-update-slice_fusion.3
  897.4 1.0 constant_dynamic-update-slice_fusion.2
  898.4 1.0 constant_dynamic-update-slice_fusion.1
  899.5 1.0 constant_dynamic-update-slice_fusion
  900.5 11.7 fusion.10
  912.2 15.2 %add_convert_fusion.10 = bf16[4,4096,512]{2,1,0:T(8,128)(2,1)} fusion(f32[4096,512]{1,0:T(8,128)} %get-tuple-element.8, f32[4]{0:T(128)S(1)} %get-tuple-element.10, f32[4096,512]{1,0:T(8,128)} %get-tuple-element.7, f32[4]{0:T(128)S(1)} %get-tuple-element.9), kind=kLoop, calls=%fused_computation.6.clone.clone.2 | loop fusion | flops 33554432 | bytes 33554464 | tf_op jit(solution)/shard_map/grk,gkc->grc/dot_general | solution.py:45
  927.4 0.0 all-to-all-done
  927.4 22.8 %copy.11 = bf16[2,16384,512]{2,1,0:T(8,128)(2,1)} copy(bf16[2,16384,512]{2,0,1:T(2,128)(2,1)} %all-to-all-done) | data formatting | bytes 67108864 | tf_op jit(solution)/shard_map/all_to_all | solution.py:40
  950.2 34.1 %slice_convert_fusion.1 = (f32[1,2048,8,512]{3,1,2,0:T(8,128)}, f32[1,2048,8,512]{3,1,2,0:T(8,128)}) fusion(bf16[2,2048,8,512]{3,1,2,0:T(8,128)(2,1)} %bitcast.25), kind=kLoop, calls=%fused_computation.8 | loop fusion | flops 16777216 | bytes 100663296 | tf_op jit(solution)/shard_map/convert_element_type | solution.py:27
  984.2 31.8 %copy.14 = f32[1,2048,8,512]{1,3,2,0:T(8,128)} copy(f32[1,2048,8,512]{3,1,2,0:T(8,128)} %get-tuple-element.6) | data formatting | bytes 67108864 | tf_op jit(solution)/shard_map/convert_element_type | solution.py:29
  1016.1 31.1 %copy.15 = f32[2048,4096]{1,0:T(8,128)} copy(f32[2048,4096]{0,1:T(8,128)} %bitcast.26) | data formatting | bytes 67108864 | tf_op jit(solution)/shard_map/convert_element_type | solution.py:29
  1047.2 31.8 %copy.12 = f32[1,2048,8,512]{1,3,2,0:T(8,128)} copy(f32[1,2048,8,512]{3,1,2,0:T(8,128)} %get-tuple-element.5) | data formatting | bytes 67108864 | tf_op jit(solution)/shard_map/convert_element_type | solution.py:27
  1079.0 31.1 %copy.13 = f32[2048,4096]{1,0:T(8,128)} copy(f32[2048,4096]{0,1:T(8,128)} %bitcast.27) | data formatting | bytes 67108864 | tf_op jit(solution)/shard_map/convert_element_type | solution.py:27
  1110.1 46.1 %fusion = f32[4,2048,512]{2,1,0:T(8,128)} fusion(f32[2048,4096]{1,0:T(8,128)} %copy.15, f32[4]{0:T(128)S(1)} %get-tuple-element.15, f32[2048,4096]{1,0:T(8,128)} %copy.13, f32[4]{0:T(128)S(1)} %get-tuple-element.16, bf16[4,4096,512]{2,1,0:T(8,128)(2,1)} %add_convert_fusion.10), kind=kOutput, calls=%fused_computation.1 | convolution fusion | flops 34493956096 | bytes 100663328 | tf_op jit(solution)/shard_map/grk,gkc->grc/dot_general | solution.py:45
  1156.2 0.0 reduce-scatter.4.cloned.1.call-update
  1156.2 175.0 %reduce-scatter.4.cloned.1.call-done = f32[1,2048,512]{2,1,0:T(8,128)} async-done(((f32[4,2048,512]{2,1,0:T(8,128)}), f32[1,2048,512]{2,1,0:T(8,128)}) %reduce-scatter.4.cloned.1.call-update) | async-done | bytes 4194320
  (3 shorter events, 0.0 us)
Async XLA Ops:
  66.6 7.3 copy-start
  66.6 799.9 %copy-start.7 = (s32[4]{0:T(128)S(1)}, s32[4]{0:T(128)}, u32[]{:S(2)}) copy-start(s32[4]{0:T(128)} %param.5) | copy-start | bytes 52
  66.6 860.8 %all-to-all-start = ((bf16[2,16384,512]{2,0,1:T(2,128)(2,1)}), bf16[2,16384,512]{2,0,1:T(2,128)(2,1)}, u32[]{:S(2)}, u32[]{:S(2)}) async-start(bf16[2,16384,512]{2,0,1:T(2,128)(2,1)} %copy.10), calls=%async_computation | async-start | bytes 67108864 | tf_op jit(solution)/shard_map/all_to_all | solution.py:40
  73.9 1257.3 %reduce-scatter.4.cloned.1.call-start = ((), (), s32[]{:S(2)}) async-start(), calls=%async_computation.2 | async-start | bytes 20971520
  73.9 556.5 %collective-permute-start = (bf16[2,512,512]{2,1,0:T(8,128)(2,1)S(1)}, bf16[2,512,512]{2,1,0:T(8,128)(2,1)S(1)}, u32[]{:S(2)}, u32[]{:S(2)}) collective-permute-start(bf16[2,512,512]{2,1,0:T(8,128)(2,1)S(1)} %copy-done), channel_id=1, source_target_pairs={{0,1},{1,2},{2,3},{3,4},{4,5},{5,6},{6,7},{7,0},{8,9},{9,10},{10,1... | collective-permute-start | bytes 3145736 | tf_op jit(solution)/shard_map/ppermute | solution.py:16
  630.4 16.1 %collective-permute-start.1 = (bf16[2,512,512]{2,1,0:T(8,128)(2,1)S(1)}, bf16[2,512,512]{2,1,0:T(8,128)(2,1)S(1)}, u32[]{:S(2)}, u32[]{:S(2)}) collective-permute-start(bf16[2,512,512]{2,1,0:T(8,128)(2,1)S(1)} %collective-permute-done), channel_id=1, source_target_pairs={{0,1},{1,2},{2,3},{3,4},{4,5},{5,6},{6,7},{7,0},{8,9},{9,10},{10,1... | collective-permute-start | bytes 3145736 | tf_op jit(solution)/shard_map/ppermute | solution.py:16
  646.5 16.1 %collective-permute-start.2 = (bf16[2,512,512]{2,1,0:T(8,128)(2,1)S(1)}, bf16[2,512,512]{2,1,0:T(8,128)(2,1)S(1)}, u32[]{:S(2)}, u32[]{:S(2)}) collective-permute-start(bf16[2,512,512]{2,1,0:T(8,128)(2,1)S(1)} %collective-permute-done.1), channel_id=1, source_target_pairs={{0,1},{1,2},{2,3},{3,4},{4,5},{5,6},{6,7},{7,0},{8,9},{9,10},{10,1... | collective-permute-start | bytes 3145736 | tf_op jit(solution)/shard_map/ppermute | solution.py:16
  662.6 1.0 copy-start.1
  663.6 160.6 %collective-permute-start.3 = (bf16[2,512,512]{2,1,0:T(8,128)(2,1)S(1)}, bf16[2,512,512]{2,1,0:T(8,128)(2,1)S(1)}, u32[]{:S(2)}, u32[]{:S(2)}) collective-permute-start(bf16[2,512,512]{2,1,0:T(8,128)(2,1)S(1)} %collective-permute-done.2), channel_id=1, source_target_pairs={{0,1},{1,2},{2,3},{3,4},{4,5},{5,6},{6,7},{7,0},{8,9},{9,10},{10,1... | collective-permute-start | bytes 3145736 | tf_op jit(solution)/shard_map/ppermute | solution.py:16
  824.2 1.0 copy-start.3
  825.2 16.4 %collective-permute-start.4 = (bf16[2,512,512]{2,1,0:T(8,128)(2,1)S(1)}, bf16[2,512,512]{2,1,0:T(8,128)(2,1)S(1)}, u32[]{:S(2)}, u32[]{:S(2)}) collective-permute-start(bf16[2,512,512]{2,1,0:T(8,128)(2,1)S(1)} %collective-permute-done.3), channel_id=1, source_target_pairs={{0,1},{1,2},{2,3},{3,4},{4,5},{5,6},{6,7},{7,0},{8,9},{9,10},{10,1... | collective-permute-start | bytes 3145736 | tf_op jit(solution)/shard_map/ppermute | solution.py:16
  841.6 1.0 copy-start.5
  842.6 16.2 %collective-permute-start.5 = (bf16[2,512,512]{2,1,0:T(8,128)(2,1)S(1)}, bf16[2,512,512]{2,1,0:T(8,128)(2,1)}, u32[]{:S(2)}, u32[]{:S(2)}) collective-permute-start(bf16[2,512,512]{2,1,0:T(8,128)(2,1)S(1)} %collective-permute-done.4), channel_id=1, source_target_pairs={{0,1},{1,2},{2,3},{3,4},{4,5},{5,6},{6,7},{7,0},{8,9},{9,10},{10,1... | collective-permute-start | bytes 3145736 | tf_op jit(solution)/shard_map/ppermute | solution.py:16
  858.8 16.4 %collective-permute-start.6 = (bf16[2,512,512]{2,1,0:T(8,128)(2,1)}, bf16[2,512,512]{2,1,0:T(8,128)(2,1)}, u32[]{:S(2)}, u32[]{:S(2)}) collective-permute-start(bf16[2,512,512]{2,1,0:T(8,128)(2,1)} %collective-permute-done.5), channel_id=1, source_target_pairs={{0,1},{1,2},{2,3},{3,4},{4,5},{5,6},{6,7},{7,0},{8,9},{9,10},{10,1... | collective-permute-start | bytes 3145736 | tf_op jit(solution)/shard_map/ppermute | solution.py:16
  866.5 27.8 %copy-start.6 = (bf16[2,512,512]{2,1,0:T(8,128)(2,1)S(1)}, bf16[2,512,512]{2,1,0:T(8,128)(2,1)}, u32[]{:S(2)}) copy-start(bf16[2,512,512]{2,1,0:T(8,128)(2,1)} %copy-done.5) | copy-start | bytes 3145732
  866.5 28.8 %copy-start.4 = (bf16[2,512,512]{2,1,0:T(8,128)(2,1)S(1)}, bf16[2,512,512]{2,1,0:T(8,128)(2,1)}, u32[]{:S(2)}) copy-start(bf16[2,512,512]{2,1,0:T(8,128)(2,1)} %copy-done.3) | copy-start | bytes 3145732
  866.5 29.9 %copy-start.2 = (bf16[2,512,512]{2,1,0:T(8,128)(2,1)S(1)}, bf16[2,512,512]{2,1,0:T(8,128)(2,1)}, u32[]{:S(2)}) copy-start(bf16[2,512,512]{2,1,0:T(8,128)(2,1)} %copy-done.1) | copy-start | bytes 3145732
Sparse Core Ops, SparseCore 0:
  1156.3 174.8 reduce-scatter.3
